TPU v7x, 256 devices: a whole 4x4x8 slice. The times are simulated.
256 devices in a mesh: seq: 64 (over z, y, core), rep: 4 (over x).
Axes of the slice: x: 4, y: 4, z: 8, core: 2. Of those that a mesh axis runs over, the one named last changes fastest.
Arguments:
- inputs: bfloat16 [4, 8192, 1024], P('rep', 'seq'), may hold values from -6 to 6
- weight_t: bfloat16 [3072, 1024], P('seq', 'rep'), may hold values from -0.1875 to 0.1875
- states: float32 [4, 8192, 1024], P('rep', 'seq'), may hold values from -0.9 to 0.9
- doc_ids: int32 [4, 8192], P('rep', 'seq'), may hold values from 0 to 31, never falling along the last dimension, each value on 1 to 512 neighbouring positions
- recur: float32 [3, 1024], replicated, may hold values from -1 to 1
- bias: float32 [3, 1024], replicated, may hold values from -8 to 3, as said below
- out_grad: bfloat16 [4, 8192, 1024], P('rep', 'seq'), may hold values from -6 to 6
Outputs:
- input_grad: bfloat16 [4, 8192, 1024], P('rep', 'seq')
- weight_grad: float32 [3072, 1024], P('seq', 'rep')
- param_grad: float32 [6, 1024], replicated
Inputs may be any that keep to these rules, and one draw needn't show every extreme that they name: `doc_ids`: within each sequence the numbers never fall; every document has 1 to 512 tokens, and some document has exactly 512. `bias`: row 0 lies between -8 and -1, rows 1 and 2 between -3 and 3.
All inputs are finite; a program needn't handle non-finite values.
Results may differ from a plain program's by a relative error of at most 0.0095.
Values may be sent and summed in bfloat16 or wider, within the bound.
No kernel may reach another device: no remote copies, remote signals or barrier semaphores. Data moves between devices by JAX's collectives and lax.ppermute only.
A program may use at most 128 MiB of HBM per device.

v0:
```python
import functools
import math
import jax
import jax.numpy as jnp
from jax import lax
from jax.sharding import Mesh
from jax.sharding import PartitionSpec as P

SEQ = ("seq_0", "seq_1", "seq_2")
SEQ_REP = ("seq_0", "seq_1", "seq_2", "rep")


def copy_for_each(x, axis):
    copies = jnp.broadcast_to(x, (lax.axis_size(axis), *x.shape))
    return lax.all_to_all(copies, axis, split_axis=0, concat_axis=0, tiled=True)


def joined_along(parts, dim):
    dims = list(parts.shape[1:])
    dims[dim] *= parts.shape[0]
    return jnp.moveaxis(parts, 0, dim).reshape(dims)


def collect(x, axis, dim):
    parts = copy_for_each(x, axis)
    return joined_along(parts, dim)


def shifted(block, axis, distance):
    devices = range(lax.axis_size(axis))
    route = [(i - distance, i) for i in devices if i - distance in devices]
    return lax.ppermute(block, axis, route)


def gathered_once(x, axis):
    leaves = jax.tree.leaves(x)
    sequence = sorted(range(len(leaves)), key=lambda k: -leaves[k].size)
    width = (1, *leaves[sequence[0]].shape)[-1]
    lines = [
        jnp.pad(leaves[k].reshape(-1), (0, -leaves[k].size % width)).reshape(-1, width)
        for k in sequence
    ]
    both, at, found = (copy_for_each(jnp.concatenate(lines), axis), 0, {})
    for k, line in zip(sequence, lines):
        piece = both[:, at : at + len(line)].reshape(len(both), -1)
        found[k] = piece[:, : leaves[k].size].reshape(-1, *leaves[k].shape)
        at += len(line)
    numbers = iter(range(len(leaves)))
    return jax.tree.map(lambda _: found[next(numbers)], x)


def combined_pairwise(pieces, combine):
    while len(jax.tree.leaves(pieces)[0]) > 1:
        pieces = jax.vmap(combine)(
            *(jax.tree.map(lambda part: part[side::2], pieces) for side in (0, 1))
        )
    return jax.tree.map(lambda part: part[0], pieces)


def carried_in(x, axis, combine, identity):
    count, here = (lax.axis_size(axis), lax.axis_index(axis))
    passed = jnp.arange(count) > here

    def kept(part, zero, own):
        part = jnp.where(
            passed.reshape(-1, *(1 for _ in own.shape)), part, jnp.asarray(zero, own.dtype)
        )
        return part[::-1]

    pieces = gathered_once(x, axis)
    return combined_pairwise(jax.tree.map(kept, pieces, identity, x), combine)


def split_up(x, dim, count):
    before, after = (x.shape[:dim], x.shape[dim + 1 :])
    return jnp.moveaxis(x.reshape(*before, count, -1, *after), dim, 0)


def sum_at_owner(x, axis, dim):
    parts = split_up(x, dim, lax.axis_size(axis))
    arrived = lax.all_to_all(parts, axis, split_axis=0, concat_axis=0, tiled=True)
    return arrived.astype(jnp.float32).sum(axis=0)


def by_axis(x, axes):
    return functools.reduce(lax.psum, axes, x)


def compose(earlier, later):
    return (later[0] * earlier[0], later[1] + later[0] * earlier[1])


def local(inputs, weight_t, states, doc_ids, recur, bias, out_grad):
    feats = inputs[0]
    hidden_now = states[0]
    ids_float = doc_ids[0].astype(jnp.float32)
    count = feats.shape[0]
    width = hidden_now.shape[1]
    columns = collect(weight_t, "rep", 1)
    contract_last = (((1,), (1,)), ((), ()))
    full_weight = lax.all_gather(columns, SEQ, axis=0, tiled=True)
    preact = lax.dot_general(feats, full_weight, contract_last, preferred_element_type=jnp.float32)
    tail_state, tail_id = shifted((hidden_now[-1:], ids_float[-1:]), SEQ, 1)
    first_same = jnp.where(
        (ids_float[0] == tail_id[0]) & (lax.axis_index(SEQ) > 0), 1.0, 0.0
    ).astype(jnp.float32)
    same = jnp.concatenate(
        [first_same[None], (ids_float[1:] == ids_float[:-1]).astype(jnp.float32)]
    )
    prior = jnp.concatenate([tail_state, hidden_now[:-1]], 0) * same[:, None]
    gate_z = jax.nn.sigmoid(preact[:, :width] + recur[0] * prior + bias[0])
    gate_r = jax.nn.sigmoid(preact[:, width : 2 * width] + recur[1] * prior + bias[1])
    gate_c = jnp.tanh(preact[:, 2 * width :] + recur[2] * gate_r * prior + bias[2])
    jacobian = same[:, None] * (
        1.0
        - gate_z
        + (gate_c - prior) * gate_z * (1.0 - gate_z) * recur[0]
        + gate_z
        * (1.0 - gate_c * gate_c)
        * recur[2]
        * (gate_r + prior * gate_r * (1.0 - gate_r) * recur[1])
    )
    upstream = out_grad[0].astype(jnp.float32)
    next_row = shifted(jacobian[:1], SEQ, -1)
    factor = jnp.concatenate([jacobian[1:], next_row], 0)
    product, local_adj = lax.associative_scan(compose, (factor, upstream), reverse=True, axis=0)
    ones_row = jnp.ones((1, width), jnp.float32)
    zeros_row = jnp.zeros((1, width), jnp.float32)
    _, entering = carried_in((product[:1], local_adj[:1]), SEQ, compose, (ones_row, zeros_row))
    adjoint = local_adj + product * entering
    grad_z = adjoint * (gate_c - prior) * gate_z * (1.0 - gate_z)
    grad_c = adjoint * gate_z * (1.0 - gate_c * gate_c)
    grad_r = grad_c * recur[2] * prior * gate_r * (1.0 - gate_r)
    grad_pre = jnp.concatenate([grad_z, grad_r, grad_c], 1).astype(jnp.bfloat16)
    input_grad = jnp.dot(grad_pre, full_weight, preferred_element_type=jnp.float32)
    tokens_all = count * inputs.shape[0] * lax.axis_size(SEQ) * lax.axis_size("rep")
    normal_factor = 1.0 / math.sqrt(tokens_all)
    row_share = lax.psum_scatter(
        lax.dot_general(
            grad_pre, feats, (((0,), (0,)), ((), ())), preferred_element_type=jnp.float32
        ),
        SEQ,
        scatter_dimension=0,
        tiled=True,
    )
    weight_grad = sum_at_owner(row_share.astype(jnp.bfloat16), "rep", 1) * normal_factor
    stats = jnp.stack(
        [
            grad_z.sum(0),
            grad_r.sum(0),
            grad_c.sum(0),
            (grad_z * prior).sum(0),
            (grad_r * prior).sum(0),
            (grad_c * gate_r * prior).sum(0),
        ]
    )
    param_grad = by_axis(stats, SEQ_REP) * normal_factor
    return (input_grad.astype(jnp.bfloat16)[None], weight_grad, param_grad)


def solution(mesh):
    torus = Mesh(
        mesh.devices.reshape(8, 4, 2, mesh.shape["rep"]), ("seq_0", "seq_1", "seq_2", "rep")
    )
    in_specs = (
        P("rep", SEQ, None),
        P(SEQ, "rep"),
        P("rep", SEQ, None),
        P("rep", SEQ),
        P(),
        P(),
        P("rep", SEQ, None),
    )
    out_specs = (P("rep", SEQ, None), P(SEQ, "rep"), P())
    return jax.shard_map(local, mesh=torus, in_specs=in_specs, out_specs=out_specs, check_vma=False)
```

profile of v0, /device:TPU:2, one launch (start us, length us, event | category | flops | bytes accessed | tf_op | source)
XLA Modules:
  0.0 406.0 jit_solution(11852315016412689403)
XLA Ops:
  8.1 9.0 %all_to_all.15 = bf16[4,48,256]{2,1,0:T(8,128)(2,1)S(1)} all-to-all(bf16[4,48,256]{2,1,0:T(8,128)(2,1)S(1)} %broadcast_in_dim.35), channel_id=1, replica_groups=mesh['seq_0'=8,'seq_1'=4,'seq_2'=2,'rep'=4] {'rep'}, dimensions={0} | all-to-all | bytes 196608 | tf_op jit(solution)/shard_map/all_to_all | solution.py:15
  18.9 1.9 collective-permute-start
  21.6 3.6 collective-permute-start.1
  27.0 1.9 fusion.33
  30.4 70.1 %all-gather.2.cloned.1.call-done = bf16[3072,1024]{1,0:T(8,128)(2,1)} async-done(((bf16[48,1024]{1,0:T(8,128)(2,1)}), bf16[3072,1024]{1,0:T(8,128)(2,1)}) %all-gather.2.cloned.1.call-update) | async-done | bytes 6291472 | tf_op jit(solution)/shard_map/all_gather | solution.py:101
  100.5 5.0 %fusion.16 = f32[128,3072]{1,0:T(8,128)S(1)} fusion(bf16[3072,1024]{1,0:T(8,128)(2,1)} %all-gather.2.cloned.1.call-done, bf16[1,128,1024]{2,1,0:T(8,128)(2,1)S(1)} %copy-done), kind=kOutput, calls=%fused_computation.39 | convolution fusion | flops 805306368 | bytes 8126464 | tf_op jit(solution)/shard_map/dot_general | solution.py:102
  111.3 4.3 %slice.416 = f32[64,1024]{1,0:T(8,128)} reverse(f32[64,1024]{1,0:T(8,128)} %slice.415), dimensions={0} | reverse | bytes 524288 | tf_op jit(solution)/shard_map/slice | solution.py:126
  115.6 4.3 %slice.420 = f32[64,1024]{1,0:T(8,128)} reverse(f32[64,1024]{1,0:T(8,128)} %slice.419), dimensions={0} | reverse | bytes 524288 | tf_op jit(solution)/shard_map/slice | solution.py:126
  120.0 4.3 %slice.391 = f32[63,1024]{1,0:T(8,128)} reverse(f32[63,1024]{1,0:T(8,128)} %slice.390), dimensions={0} | reverse | bytes 516096 | tf_op jit(solution)/shard_map/slice | solution.py:126
  125.5 4.3 %slice.418 = f32[64,1024]{1,0:T(8,128)} reverse(f32[64,1024]{1,0:T(8,128)} %slice.417), dimensions={0} | reverse | bytes 524288 | tf_op jit(solution)/shard_map/slice | solution.py:126
  129.8 2.5 slice.424
  143.5 1.4 fusion.37
  151.8 1.4 fusion.40
  158.4 1.4 fusion.39
  159.9 1.4 slice.444
  169.5 2.5 slice.414
  183.1 1.7 pad_maximum_fusion.5
  184.8 2.6 pad.112
  187.5 2.6 pad.113
  191.9 9.2 %all-to-all-start.1 = ((f32[64,2,1024]{2,1,0:T(2,128)}), f32[64,2,1024]{2,1,0:T(2,128)}, u32[]{:S(2)}, u32[]{:S(2)}) async-start(f32[64,2,1024]{2,1,0:T(2,128)} %broadcast_in_dim.37), calls=%async_computation.1 | async-start | bytes 1048576 | tf_op jit(solution)/shard_map/all_to_all | solution.py:15
  204.1 3.4 rev.5
  207.6 10.9 %all-to-all-done.1 = f32[64,2,1024]{2,1,0:T(2,128)} async-done(((f32[64,2,1024]{2,1,0:T(2,128)}), f32[64,2,1024]{2,1,0:T(2,128)}, u32[]{:S(2)}, u32[]{:S(2)}) %all-to-all-start.1) | async-done | bytes 524320 | tf_op jit(solution)/shard_map/all_to_all | solution.py:15
  218.5 1.9 broadcast_select_fusion
  223.1 6.4 %fusion.13 = f32[3072,1024]{1,0:T(8,128)} fusion(bf16[128,1024]{1,0:T(8,128)(2,1)S(1)} %get-tuple-element.11, bf16[128,1024]{1,0:T(8,128)(2,1)S(1)} %get-tuple-element.10, bf16[128,1024]{1,0:T(8,128)(2,1)S(1)} %get-tuple-element.9, bf16[1,128,1024]{2,1,0:T(8,128)(2,1)S(1)} %copy-done), kind=kOutput, calls=%fused_computation.32 | convolution fusion | flops 807665664 | bytes 13631488 | tf_op jit(solution)/shard_map/dot_general | solution.py:139
  229.5 28.7 %psum.28 = f32[6,1024]{1,0:T(8,128)S(1)} all-reduce(f32[6,1024]{1,0:T(8,128)S(1)} %stack.27), channel_id=1, replica_groups=mesh['seq_0'=8,'seq_1'=4,'seq_2'=2,'rep'=4] {'seq_0'}, use_global_device_ids=true, to_apply=%region_8.9 | all-reduce | flops 6144 | bytes 49152 | tf_op jit(solution)/shard_map/psum | solution.py:86
  258.3 16.3 %psum.29 = f32[6,1024]{1,0:T(8,128)S(1)} all-reduce(f32[6,1024]{1,0:T(8,128)S(1)} %psum.28), channel_id=1, replica_groups=mesh['seq_0'=8,'seq_1'=4,'seq_2'=2,'rep'=4] {'seq_1'}, use_global_device_ids=true, to_apply=%region_9.10 | all-reduce | flops 6144 | bytes 49152 | tf_op jit(solution)/shard_map/psum | solution.py:86
  274.6 3.4 psum.30
  278.0 14.1 %psum.31 = f32[6,1024]{1,0:T(8,128)S(1)} all-reduce(f32[6,1024]{1,0:T(8,128)S(1)} %psum.30), channel_id=1, replica_groups=mesh['seq_0'=8,'seq_1'=4,'seq_2'=2,'rep'=4] {'rep'}, use_global_device_ids=true, to_apply=%region_11.12 | all-reduce | flops 6144 | bytes 49152 | tf_op jit(solution)/shard_map/psum | solution.py:86
  292.1 4.6 %fusion = bf16[1,128,1024]{2,1,0:T(8,128)(2,1)} fusion(bf16[3072,1024]{1,0:T(8,128)(2,1)} %all-gather.2.cloned.1.call-done, bf16[128,1024]{1,0:T(8,128)(2,1)S(1)} %copy-done.9, bf16[128,1024]{1,0:T(8,128)(2,1)S(1)} %copy-done.7, bf16[128,1024]{1,0:T(8,128)(2,1)S(1)} %copy-done.5), kind=kOutput, calls=%fused_computation.1 | convolution fusion | flops 807796736 | bytes 7340032 | tf_op jit(solution)/shard_map/dot_general | solution.py:135
  296.7 91.0 %reduce-scatter.2.cloned.1.call-done = f32[48,1024]{1,0:T(8,128)} async-done(((f32[3072,1024]{1,0:T(8,128)}), f32[48,1024]{1,0:T(8,128)}) %reduce-scatter.2.cloned.1.call-update) | async-done | bytes 196624 | tf_op jit(solution)/shard_map/reduce_scatter | solution.py:138
  389.3 4.8 %all-to-all-start.2 = ((bf16[4,48,256]{2,1,0:T(8,128)(2,1)}), bf16[4,48,256]{2,1,0:T(8,128)(2,1)S(1)}, u32[]{:S(2)}, u32[]{:S(2)}) async-start(bf16[4,48,256]{2,1,0:T(8,128)(2,1)} %bitcast.45), calls=%async_computation.3 | async-start | bytes 196608 | tf_op jit(solution)/shard_map/all_to_all | solution.py:81
  394.7 3.7 all-to-all-done.2
  (222 shorter events, 64.8 us)
Async XLA Ops:
  7.2 93.3 %copy-start = (bf16[1,128,1024]{2,1,0:T(8,128)(2,1)S(1)}, bf16[1,128,1024]{2,1,0:T(8,128)(2,1)}, u32[]{:S(2)}) copy-start(bf16[1,128,1024]{2,1,0:T(8,128)(2,1)} %param.7) | copy-start | bytes 786436
  7.2 21.7 %copy-start.12 = (f32[1,128,1024]{2,1,0:T(8,128)S(1)}, f32[1,128,1024]{2,1,0:T(8,128)}, u32[]{:S(2)}) copy-start(f32[1,128,1024]{2,1,0:T(8,128)} %param.9) | copy-start | bytes 1572868
  7.2 93.3 %all-gather.2.cloned.1.call-start = ((), (), s32[]{:S(2)}) async-start(), calls=%async_computation.4 | async-start | bytes 6389760 | tf_op jit(solution)/shard_map/all_gather | solution.py:101
  18.9 10.0 %collective-permute-start = (f32[1]{0:T(128)}, f32[1]{0:T(128)}, u32[]{:S(2)}, u32[]{:S(2)}) collective-permute-start(f32[1]{0:T(128)} %bitcast.3), channel_id=1, source_target_pairs={{0,4},{4,8},{8,12},{12,16},{16,20},{20,24},{24,28},{28,32},{32,36}... | collective-permute-start | bytes 20 | tf_op jit(solution)/shard_map/ppermute | solution.py:32
  21.6 83.9 %collective-permute-start.1 = (f32[1,1024]{1,0:T(1,128)S(1)}, f32[1,1024]{1,0:T(1,128)S(1)}, u32[]{:S(2)}, u32[]{:S(2)}) collective-permute-start(f32[1,1024]{1,0:T(1,128)S(1)} %slice_bitcast_fusion.2), channel_id=1, source_target_pairs={{0,4},{4,8},{8,12},{12,16},{16,20},{20,24},{24,28},{28,32},{32,36}... | collective-permute-start | bytes 12296 | tf_op jit(solution)/shard_map/ppermute | solution.py:32
  26.1 79.3 %copy-start.16 = (f32[1,1024]{1,0:T(1,128)}, f32[1,1024]{1,0:T(1,128)S(1)}, u32[]{:S(2)}) copy-start(f32[1,1024]{1,0:T(1,128)S(1)} %get-tuple-element.58) | copy-start | bytes 12292
  26.1 79.3 %copy-start.18 = (f32[1,1024]{1,0:T(1,128)}, f32[1,1024]{1,0:T(1,128)S(1)}, u32[]{:S(2)}) copy-start(f32[1,1024]{1,0:T(1,128)S(1)} %get-tuple-element.59) | copy-start | bytes 12292
  26.1 79.3 %copy-start.20 = (f32[1,1024]{1,0:T(1,128)}, f32[1,1024]{1,0:T(1,128)S(1)}, u32[]{:S(2)}) copy-start(f32[1,1024]{1,0:T(1,128)S(1)} %get-tuple-element.60) | copy-start | bytes 12292
  27.0 78.5 %copy-start.22 = (f32[1,1024]{1,0:T(1,128)}, f32[1,1024]{1,0:T(1,128)S(1)}, u32[]{:S(2)}) copy-start(f32[1,1024]{1,0:T(1,128)S(1)} %get-tuple-element.55) | copy-start | bytes 12292
  27.0 78.5 %copy-start.24 = (f32[1,1024]{1,0:T(1,128)}, f32[1,1024]{1,0:T(1,128)S(1)}, u32[]{:S(2)}) copy-start(f32[1,1024]{1,0:T(1,128)S(1)} %get-tuple-element.56) | copy-start | bytes 12292
  27.0 78.5 %copy-start.26 = (f32[1,1024]{1,0:T(1,128)}, f32[1,1024]{1,0:T(1,128)S(1)}, u32[]{:S(2)}) copy-start(f32[1,1024]{1,0:T(1,128)S(1)} %get-tuple-element.57) | copy-start | bytes 12292
  30.4 75.1 %copy-start.39 = (f32[128]{0:T(128)}, f32[128]{0:T(128)S(1)}, u32[]{:S(2)}) copy-start(f32[128]{0:T(128)S(1)} %pad_maximum_fusion.17) | copy-start | bytes 1540
  105.5 4.3 %copy-start.37 = (f32[1,1024]{1,0:T(1,128)}, f32[1,1024]{1,0:T(1,128)S(1)}, u32[]{:S(2)}) copy-start(f32[1,1024]{1,0:T(1,128)S(1)} %collective-permute-done.1) | copy-start | bytes 12292
  106.3 18.0 %collective-permute-start.2 = (f32[1,1024]{1,0:T(1,128)S(1)}, f32[1,1024]{1,0:T(1,128)S(1)}, u32[]{:S(2)}, u32[]{:S(2)}) collective-permute-start(f32[1,1024]{1,0:T(1,128)S(1)} %slice.515), channel_id=1, source_target_pairs={{4,0},{8,4},{12,8},{16,12},{20,16},{24,20},{28,24},{32,28},{36,32}... | collective-permute-start | bytes 12296 | tf_op jit(solution)/shard_map/ppermute | solution.py:32
  124.4 5.5 %copy-start.28 = (f32[1,1024]{1,0:T(1,128)}, f32[1,1024]{1,0:T(1,128)S(1)}, u32[]{:S(2)}) copy-start(f32[1,1024]{1,0:T(1,128)S(1)} %collective-permute-done.2) | copy-start | bytes 12292
  159.9 14.4 %copy-start.15 = (f32[3,1024]{1,0:T(4,128)S(1)}, f32[3,1024]{1,0:T(4,128)}, u32[]{:S(2)}) copy-start(f32[3,1024]{1,0:T(4,128)} %slice.446) | copy-start | bytes 36868
  168.3 9.2 %copy-start.13 = (f32[15,1024]{1,0:T(8,128)S(1)}, f32[15,1024]{1,0:T(8,128)}, u32[]{:S(2)}) copy-start(f32[15,1024]{1,0:T(8,128)} %slice.432) | copy-start | bytes 184324
  168.3 9.2 %copy-start.14 = (f32[15,1024]{1,0:T(8,128)S(1)}, f32[15,1024]{1,0:T(8,128)}, u32[]{:S(2)}) copy-start(f32[15,1024]{1,0:T(8,128)} %slice.430) | copy-start | bytes 184324
  168.9 8.4 %copy-start.36 = (f32[1,1024]{1,0:T(1,128)S(1)}, f32[1,1024]{1,0:T(1,128)}, u32[]{:S(2)}) copy-start(f32[1,1024]{1,0:T(1,128)} %slice.540) | copy-start | bytes 12292
  168.9 8.5 %copy-start.35 = (f32[1,1024]{1,0:T(1,128)S(1)}, f32[1,1024]{1,0:T(1,128)}, u32[]{:S(2)}) copy-start(f32[1,1024]{1,0:T(1,128)} %slice.518) | copy-start | bytes 12292
  168.9 8.6 %copy-start.34 = (f32[1,1024]{1,0:T(1,128)S(1)}, f32[1,1024]{1,0:T(1,128)}, u32[]{:S(2)}) copy-start(f32[1,1024]{1,0:T(1,128)} %slice.539) | copy-start | bytes 12292
  179.6 1.5 copy-start.10
  179.7 1.5 copy-start.11
  180.4 1.6 copy-start.30
  191.9 26.6 %all-to-all-start.1 = ((f32[64,2,1024]{2,1,0:T(2,128)}), f32[64,2,1024]{2,1,0:T(2,128)}, u32[]{:S(2)}, u32[]{:S(2)}) async-start(f32[64,2,1024]{2,1,0:T(2,128)} %broadcast_in_dim.37), calls=%async_computation.1 | async-start | bytes 1048576 | tf_op jit(solution)/shard_map/all_to_all | solution.py:15
  201.1 186.7 %reduce-scatter.2.cloned.1.call-start = ((), (), s32[]{:S(2)}) async-start(), calls=%async_computation.5 | async-start | bytes 12779520 | tf_op jit(solution)/shard_map/reduce_scatter | solution.py:138
  201.3 1.4 copy-start.2
  202.7 1.2 copy-start.3
  229.5 62.6 %copy-start.5 = (bf16[128,1024]{1,0:T(8,128)(2,1)S(1)}, bf16[128,1024]{1,0:T(8,128)(2,1)}, u32[]{:S(2)}) copy-start(bf16[128,1024]{1,0:T(8,128)(2,1)} %copy-done.4) | copy-start | bytes 786436
  229.5 62.6 %copy-start.7 = (bf16[128,1024]{1,0:T(8,128)(2,1)S(1)}, bf16[128,1024]{1,0:T(8,128)(2,1)}, u32[]{:S(2)}) copy-start(bf16[128,1024]{1,0:T(8,128)(2,1)} %copy-done.6) | copy-start | bytes 786436
  229.5 62.6 %copy-start.9 = (bf16[128,1024]{1,0:T(8,128)(2,1)S(1)}, bf16[128,1024]{1,0:T(8,128)(2,1)}, u32[]{:S(2)}) copy-start(bf16[128,1024]{1,0:T(8,128)(2,1)} %copy-done.8) | copy-start | bytes 786436
  389.3 9.2 %all-to-all-start.2 = ((bf16[4,48,256]{2,1,0:T(8,128)(2,1)}), bf16[4,48,256]{2,1,0:T(8,128)(2,1)S(1)}, u32[]{:S(2)}, u32[]{:S(2)}) async-start(bf16[4,48,256]{2,1,0:T(8,128)(2,1)} %bitcast.45), calls=%async_computation.3 | async-start | bytes 196608 | tf_op jit(solution)/shard_map/all_to_all | solution.py:81
  (16 other events, 13.7 us)
Sparse Core Ops, SparseCore 0:
  17.8 82.6 all-gather.1
  229.6 158.0 reduce-scatter.1
where the time goes:
time: 410 us; the launch traced here: 406 us
  waiting for transfers between devices  176 us (43%)
  local copies, waits for them, and re-layouts  75.4 us (18%)
  blocking collectives  71.5 us (17%)
  other arithmetic  30 us (7%)
  starting transfers between devices  21 us (5%)
  between operations  16.4 us (4%)
  matrix products  16 us (4%)
    reduce_scatter x1, waiting for transfers between devices, local(): lax.psum_scatter(lax.dot_general(grad_pre, feats, (((0,), (0,)), ((), ())...  91 us
    all_gather x1, waiting for transfers between devices, local(): full_weight = lax.all_gather(columns, SEQ, axis=0, tiled=True)  70.1 us
    psum x4, blocking collectives, by_axis(): return functools.reduce(lax.psum, axes, x)  62.5 us
    slice x49, local copies, waits for them, and re-layouts, local(): lax.associative_scan(compose, (factor, upstream), reverse=True, axis=0)  55.3 us
    all_to_all x1, waiting for transfers between devices, copy_for_each(): return lax.all_to_all(copies, axis, split_axis=0, concat_axis=0, tiled=True)  10.9 us
    mul x16, other arithmetic, compose(): return (later[0] * earlier[0], later[1] + later[0] * earlier[1])  10.4 us
    all_to_all x1, starting transfers between devices, copy_for_each(): return lax.all_to_all(copies, axis, split_axis=0, concat_axis=0, tiled=True)  9.17 us
    all_to_all x1, blocking collectives, copy_for_each(): return lax.all_to_all(copies, axis, split_axis=0, concat_axis=0, tiled=True)  8.96 us
  transfers between devices with their start and end apart: 7, of which 4 were waited for; matrix products, arithmetic and copies ran while one was open for 9% of the time, Pallas kernels for 0%

commit v1 on v0

--- a/solution.py
+++ b/solution.py
@@ -98,7 +98,9 @@
     width = hidden_now.shape[1]
     columns = collect(weight_t, "rep", 1)
     contract_last = (((1,), (1,)), ((), ()))
-    full_weight = lax.all_gather(columns, SEQ, axis=0, tiled=True)
+    full_weight = jnp.concatenate(
+        lax.all_to_all(jnp.stack([columns] * lax.axis_size(SEQ)), SEQ, 0, 0), axis=0
+    )
     preact = lax.dot_general(feats, full_weight, contract_last, preferred_element_type=jnp.float32)
     tail_state, tail_id = shifted((hidden_now[-1:], ids_float[-1:]), SEQ, 1)
     first_same = jnp.where(

time: 410 us -> 481 us (1.17)
  waiting for transfers between devices: 176 us -> 237 us
  starting transfers between devices: 21 us -> 32 us
    all_to_all x0 -> x1, waiting for transfers between devices: none -> 133 us  [local(): lax.all_to_all(jnp.stack([columns] * lax.axis_size(SEQ)), SEQ, 0, 0)]
    all_gather x1 -> x0, waiting for transfers between devices: 70.1 us -> none  [local(): full_weight = lax.all_gather(columns, SEQ, axis=0, tiled=True)]
    all_to_all x0 -> x1, starting transfers between devices: none -> 12.5 us  [local(): lax.all_to_all(jnp.stack([columns] * lax.axis_size(SEQ)), SEQ, 0, 0)]
  transfers between devices with their start and end apart: 7 -> 7, of which waited for: 4 -> 4; matrix products, arithmetic and copies ran while one was open for 9% -> 7% of each run, Pallas kernels for 0% -> 0%
where the time goes in v1:
time: 481 us; the launch traced here: 477 us
  waiting for transfers between devices  237 us (49%)
  local copies, waits for them, and re-layouts  75.8 us (16%)
  blocking collectives  72 us (15%)
  starting transfers between devices  32 us (7%)
  other arithmetic  28.3 us (6%)
  between operations  16.5 us (3%)
  matrix products  15.9 us (3%)
    all_to_all x1, waiting for transfers between devices, local(): lax.all_to_all(jnp.stack([columns] * lax.axis_size(SEQ)), SEQ, 0, 0)  133 us
    reduce_scatter x1, waiting for transfers between devices, local(): lax.psum_scatter(lax.dot_general(grad_pre, feats, (((0,), (0,)), ((), ())...  89.7 us
    psum x4, blocking collectives, by_axis(): return functools.reduce(lax.psum, axes, x)  63 us
    slice x49, local copies, waits for them, and re-layouts, local(): lax.associative_scan(compose, (factor, upstream), reverse=True, axis=0)  55.3 us
    all_to_all x1, starting transfers between devices, local(): lax.all_to_all(jnp.stack([columns] * lax.axis_size(SEQ)), SEQ, 0, 0)  12.5 us
    all_to_all x1, waiting for transfers between devices, copy_for_each(): return lax.all_to_all(copies, axis, split_axis=0, concat_axis=0, tiled=True)  10.9 us
    mul x16, other arithmetic, compose(): return (later[0] * earlier[0], later[1] + later[0] * earlier[1])  10.4 us
  transfers between devices with their start and end apart: 7, of which 4 were waited for; matrix products, arithmetic and copies ran while one was open for 7% of the time, Pallas kernels for 0%

profile of v1, /device:TPU:2, one launch (start us, length us, event | category | flops | bytes accessed | tf_op | source)
XLA Modules:
  0.0 477.3 jit_solution(725182742763746214)
XLA Ops:
  8.0 9.0 %all_to_all.20 = bf16[4,48,256]{2,1,0:T(8,128)(2,1)S(1)} all-to-all(bf16[4,48,256]{2,1,0:T(8,128)(2,1)S(1)} %broadcast_in_dim.35), channel_id=1, replica_groups=mesh['seq_0'=8,'seq_1'=4,'seq_2'=2,'rep'=4] {'rep'}, dimensions={0} | all-to-all | bytes 196608 | tf_op jit(solution)/shard_map/all_to_all | solution.py:15
  16.9 3.5 stack.24
  20.4 12.5 %all-to-all-start.1 = ((bf16[64,48,1024]{2,1,0:T(8,128)(2,1)}), bf16[64,48,1024]{2,1,0:T(8,128)(2,1)}, u32[]{:S(2)}, u32[]{:S(2)}) async-start(bf16[64,48,1024]{2,1,0:T(8,128)(2,1)} %stack.24), calls=%async_computation.1 | async-start | bytes 12582912 | tf_op jit(solution)/shard_map/all_to_all | solution.py:102
  33.5 2.5 collective-permute-start
  36.0 3.0 collective-permute-start.1
  41.6 132.6 %all-to-all-done.1 = bf16[64,48,1024]{2,1,0:T(8,128)(2,1)} async-done(((bf16[64,48,1024]{2,1,0:T(8,128)(2,1)}), bf16[64,48,1024]{2,1,0:T(8,128)(2,1)}, u32[]{:S(2)}, u32[]{:S(2)}) %all-to-all-start.1) | async-done | bytes 6291488 | tf_op jit(solution)/shard_map/all_to_all | solution.py:102
  174.2 5.0 %fusion.16 = f32[128,3072]{1,0:T(8,128)S(1)} fusion(bf16[3072,1024]{1,0:T(8,128)(2,1)} %bitcast.9, bf16[1,128,1024]{2,1,0:T(8,128)(2,1)S(1)} %copy-done), kind=kOutput, calls=%fused_computation.39 | convolution fusion | flops 805306368 | bytes 8126464 | tf_op jit(solution)/shard_map/dot_general | solution.py:104
  185.0 4.3 slice.416
  189.4 4.3 slice.420
  193.7 4.4 slice.391
  199.2 4.3 slice.418
  203.6 2.5 slice.424
  217.2 1.4 fusion.37
  225.5 1.4 fusion.40
  232.1 1.4 fusion.39
  243.2 2.5 slice.414
  256.8 1.7 pad_maximum_fusion.5
  258.5 2.7 pad.112
  261.2 2.7 pad.113
  265.6 7.8 %all-to-all-start.2 = ((f32[64,2,1024]{2,1,0:T(2,128)}), f32[64,2,1024]{2,1,0:T(2,128)}, u32[]{:S(2)}, u32[]{:S(2)}) async-start(f32[64,2,1024]{2,1,0:T(2,128)} %broadcast_in_dim.37), calls=%async_computation.2 | async-start | bytes 1048576 | tf_op jit(solution)/shard_map/all_to_all | solution.py:15
  276.5 3.4 rev.5
  279.9 10.9 %all-to-all-done.2 = f32[64,2,1024]{2,1,0:T(2,128)} async-done(((f32[64,2,1024]{2,1,0:T(2,128)}), f32[64,2,1024]{2,1,0:T(2,128)}, u32[]{:S(2)}, u32[]{:S(2)}) %all-to-all-start.2) | async-done | bytes 524320 | tf_op jit(solution)/shard_map/all_to_all | solution.py:15
  290.8 1.8 broadcast_select_fusion
  295.4 6.4 %fusion.13 = f32[3072,1024]{1,0:T(8,128)} fusion(bf16[128,1024]{1,0:T(8,128)(2,1)S(1)} %get-tuple-element.11, bf16[128,1024]{1,0:T(8,128)(2,1)S(1)} %get-tuple-element.10, bf16[128,1024]{1,0:T(8,128)(2,1)S(1)} %get-tuple-element.9, bf16[1,128,1024]{2,1,0:T(8,128)(2,1)S(1)} %copy-done), kind=kOutput, calls=%fused_computation.32 | convolution fusion | flops 807665664 | bytes 13631488 | tf_op jit(solution)/shard_map/dot_general | solution.py:141
  301.8 28.7 %psum.28 = f32[6,1024]{1,0:T(8,128)S(1)} all-reduce(f32[6,1024]{1,0:T(8,128)S(1)} %stack.31), channel_id=1, replica_groups=mesh['seq_0'=8,'seq_1'=4,'seq_2'=2,'rep'=4] {'seq_0'}, use_global_device_ids=true, to_apply=%region_8.9 | all-reduce | flops 6144 | bytes 49152 | tf_op jit(solution)/shard_map/psum | solution.py:86
  330.6 16.3 %psum.29 = f32[6,1024]{1,0:T(8,128)S(1)} all-reduce(f32[6,1024]{1,0:T(8,128)S(1)} %psum.28), channel_id=1, replica_groups=mesh['seq_0'=8,'seq_1'=4,'seq_2'=2,'rep'=4] {'seq_1'}, use_global_device_ids=true, to_apply=%region_9.10 | all-reduce | flops 6144 | bytes 49152 | tf_op jit(solution)/shard_map/psum | solution.py:86
  346.9 3.4 psum.30
  350.3 14.6 %psum.31 = f32[6,1024]{1,0:T(8,128)S(1)} all-reduce(f32[6,1024]{1,0:T(8,128)S(1)} %psum.30), channel_id=1, replica_groups=mesh['seq_0'=8,'seq_1'=4,'seq_2'=2,'rep'=4] {'rep'}, use_global_device_ids=true, to_apply=%region_11.12 | all-reduce | flops 6144 | bytes 49152 | tf_op jit(solution)/shard_map/psum | solution.py:86
  364.9 4.5 fusion
  369.4 89.7 %reduce-scatter.2.cloned.1.call-done = f32[48,1024]{1,0:T(8,128)} async-done(((f32[3072,1024]{1,0:T(8,128)}), f32[48,1024]{1,0:T(8,128)}) %reduce-scatter.2.cloned.1.call-update) | async-done | bytes 196624 | tf_op jit(solution)/shard_map/reduce_scatter | solution.py:140
  460.7 4.8 %all-to-all-start.3 = ((bf16[4,48,256]{2,1,0:T(8,128)(2,1)}), bf16[4,48,256]{2,1,0:T(8,128)(2,1)S(1)}, u32[]{:S(2)}, u32[]{:S(2)}) async-start(bf16[4,48,256]{2,1,0:T(8,128)(2,1)} %bitcast.46), calls=%async_computation.4 | async-start | bytes 196608 | tf_op jit(solution)/shard_map/all_to_all | solution.py:81
  466.1 3.7 all-to-all-done.3
  (230 shorter events, 63.2 us)
Async XLA Ops:
  7.2 167.1 %copy-start = (bf16[1,128,1024]{2,1,0:T(8,128)(2,1)S(1)}, bf16[1,128,1024]{2,1,0:T(8,128)(2,1)}, u32[]{:S(2)}) copy-start(bf16[1,128,1024]{2,1,0:T(8,128)(2,1)} %param.7) | copy-start | bytes 786436
  20.4 12.5 %copy-start.44 = (s32[1,128]{1,0:T(1,128)S(1)}, s32[1,128]{1,0:T(1,128)}, u32[]{:S(2)}) copy-start(s32[1,128]{1,0:T(1,128)} %param.10) | copy-start | bytes 1540
  20.4 15.6 %copy-start.12 = (f32[1,128,1024]{2,1,0:T(8,128)S(1)}, f32[1,128,1024]{2,1,0:T(8,128)}, u32[]{:S(2)}) copy-start(f32[1,128,1024]{2,1,0:T(8,128)} %param.9) | copy-start | bytes 1572868
  20.4 18.7 %copy-start.40 = (f32[3,1024]{1,0:T(4,128)S(1)}, f32[3,1024]{1,0:T(4,128)}, u32[]{:S(2)}) copy-start(f32[3,1024]{1,0:T(4,128)} %param.12) | copy-start | bytes 36868
  20.4 18.7 %copy-start.41 = (f32[3,1024]{1,0:T(4,128)S(1)}, f32[3,1024]{1,0:T(4,128)}, u32[]{:S(2)}) copy-start(f32[3,1024]{1,0:T(4,128)} %param.11) | copy-start | bytes 36868
  20.4 18.7 %copy-start.13 = (bf16[1,128,1024]{2,1,0:T(8,128)(2,1)S(1)}, bf16[1,128,1024]{2,1,0:T(8,128)(2,1)}, u32[]{:S(2)}) copy-start(bf16[1,128,1024]{2,1,0:T(8,128)(2,1)} %param.13) | copy-start | bytes 786436
  20.4 153.8 %all-to-all-start.1 = ((bf16[64,48,1024]{2,1,0:T(8,128)(2,1)}), bf16[64,48,1024]{2,1,0:T(8,128)(2,1)}, u32[]{:S(2)}, u32[]{:S(2)}) async-start(bf16[64,48,1024]{2,1,0:T(8,128)(2,1)} %stack.24), calls=%async_computation.1 | async-start | bytes 12582912 | tf_op jit(solution)/shard_map/all_to_all | solution.py:102
  33.5 6.6 %collective-permute-start = (f32[1]{0:T(128)}, f32[1]{0:T(128)}, u32[]{:S(2)}, u32[]{:S(2)}) collective-permute-start(f32[1]{0:T(128)} %bitcast.3), channel_id=1, source_target_pairs={{0,4},{4,8},{8,12},{12,16},{16,20},{20,24},{24,28},{28,32},{32,36}... | collective-permute-start | bytes 20 | tf_op jit(solution)/shard_map/ppermute | solution.py:32
  36.0 143.2 %collective-permute-start.1 = (f32[1,1024]{1,0:T(1,128)S(1)}, f32[1,1024]{1,0:T(1,128)S(1)}, u32[]{:S(2)}, u32[]{:S(2)}) collective-permute-start(f32[1,1024]{1,0:T(1,128)S(1)} %slice_bitcast_fusion.2), channel_id=1, source_target_pairs={{0,4},{4,8},{8,12},{12,16},{16,20},{20,24},{24,28},{28,32},{32,36}... | collective-permute-start | bytes 12296 | tf_op jit(solution)/shard_map/ppermute | solution.py:32
  39.1 140.1 %copy-start.17 = (f32[1,1024]{1,0:T(1,128)}, f32[1,1024]{1,0:T(1,128)S(1)}, u32[]{:S(2)}) copy-start(f32[1,1024]{1,0:T(1,128)S(1)} %get-tuple-element.58) | copy-start | bytes 12292
  39.1 140.1 %copy-start.19 = (f32[1,1024]{1,0:T(1,128)}, f32[1,1024]{1,0:T(1,128)S(1)}, u32[]{:S(2)}) copy-start(f32[1,1024]{1,0:T(1,128)S(1)} %get-tuple-element.59) | copy-start | bytes 12292
  39.1 140.1 %copy-start.21 = (f32[1,1024]{1,0:T(1,128)}, f32[1,1024]{1,0:T(1,128)S(1)}, u32[]{:S(2)}) copy-start(f32[1,1024]{1,0:T(1,128)S(1)} %get-tuple-element.60) | copy-start | bytes 12292
  39.2 140.1 %copy-start.23 = (f32[1,1024]{1,0:T(1,128)}, f32[1,1024]{1,0:T(1,128)S(1)}, u32[]{:S(2)}) copy-start(f32[1,1024]{1,0:T(1,128)S(1)} %get-tuple-element.55) | copy-start | bytes 12292
  39.2 140.1 %copy-start.25 = (f32[1,1024]{1,0:T(1,128)}, f32[1,1024]{1,0:T(1,128)S(1)}, u32[]{:S(2)}) copy-start(f32[1,1024]{1,0:T(1,128)S(1)} %get-tuple-element.56) | copy-start | bytes 12292
  39.2 140.1 %copy-start.27 = (f32[1,1024]{1,0:T(1,128)}, f32[1,1024]{1,0:T(1,128)S(1)}, u32[]{:S(2)}) copy-start(f32[1,1024]{1,0:T(1,128)S(1)} %get-tuple-element.57) | copy-start | bytes 12292
  41.6 137.7 %copy-start.42 = (f32[128]{0:T(128)}, f32[128]{0:T(128)S(1)}, u32[]{:S(2)}) copy-start(f32[128]{0:T(128)S(1)} %pad_maximum_fusion.17) | copy-start | bytes 1540
  179.2 4.3 copy-start.38
  180.1 18.0 %collective-permute-start.2 = (f32[1,1024]{1,0:T(1,128)S(1)}, f32[1,1024]{1,0:T(1,128)S(1)}, u32[]{:S(2)}, u32[]{:S(2)}) collective-permute-start(f32[1,1024]{1,0:T(1,128)S(1)} %slice.515), channel_id=1, source_target_pairs={{4,0},{8,4},{12,8},{16,12},{20,16},{24,20},{28,24},{32,28},{36,32}... | collective-permute-start | bytes 12296 | tf_op jit(solution)/shard_map/ppermute | solution.py:32
  198.1 5.5 %copy-start.29 = (f32[1,1024]{1,0:T(1,128)}, f32[1,1024]{1,0:T(1,128)S(1)}, u32[]{:S(2)}) copy-start(f32[1,1024]{1,0:T(1,128)S(1)} %collective-permute-done.2) | copy-start | bytes 12292
  233.5 14.4 %copy-start.16 = (f32[3,1024]{1,0:T(4,128)S(1)}, f32[3,1024]{1,0:T(4,128)}, u32[]{:S(2)}) copy-start(f32[3,1024]{1,0:T(4,128)} %slice.446) | copy-start | bytes 36868
  242.0 9.2 %copy-start.14 = (f32[15,1024]{1,0:T(8,128)S(1)}, f32[15,1024]{1,0:T(8,128)}, u32[]{:S(2)}) copy-start(f32[15,1024]{1,0:T(8,128)} %slice.432) | copy-start | bytes 184324
  242.0 9.2 %copy-start.15 = (f32[15,1024]{1,0:T(8,128)S(1)}, f32[15,1024]{1,0:T(8,128)}, u32[]{:S(2)}) copy-start(f32[15,1024]{1,0:T(8,128)} %slice.430) | copy-start | bytes 184324
  242.6 8.4 %copy-start.37 = (f32[1,1024]{1,0:T(1,128)S(1)}, f32[1,1024]{1,0:T(1,128)}, u32[]{:S(2)}) copy-start(f32[1,1024]{1,0:T(1,128)} %slice.540) | copy-start | bytes 12292
  242.6 8.5 %copy-start.36 = (f32[1,1024]{1,0:T(1,128)S(1)}, f32[1,1024]{1,0:T(1,128)}, u32[]{:S(2)}) copy-start(f32[1,1024]{1,0:T(1,128)} %slice.518) | copy-start | bytes 12292
  242.6 8.6 %copy-start.35 = (f32[1,1024]{1,0:T(1,128)S(1)}, f32[1,1024]{1,0:T(1,128)}, u32[]{:S(2)}) copy-start(f32[1,1024]{1,0:T(1,128)} %slice.539) | copy-start | bytes 12292
  254.1 1.6 copy-start.31
  265.6 25.2 %all-to-all-start.2 = ((f32[64,2,1024]{2,1,0:T(2,128)}), f32[64,2,1024]{2,1,0:T(2,128)}, u32[]{:S(2)}, u32[]{:S(2)}) async-start(f32[64,2,1024]{2,1,0:T(2,128)} %broadcast_in_dim.37), calls=%async_computation.2 | async-start | bytes 1048576 | tf_op jit(solution)/shard_map/all_to_all | solution.py:15
  273.4 185.7 %reduce-scatter.2.cloned.1.call-start = ((), (), s32[]{:S(2)}) async-start(), calls=%async_computation.5 | async-start | bytes 12779520 | tf_op jit(solution)/shard_map/reduce_scatter | solution.py:140
  301.8 63.1 %copy-start.5 = (bf16[128,1024]{1,0:T(8,128)(2,1)S(1)}, bf16[128,1024]{1,0:T(8,128)(2,1)}, u32[]{:S(2)}) copy-start(bf16[128,1024]{1,0:T(8,128)(2,1)} %copy-done.4) | copy-start | bytes 786436
  301.8 63.1 %copy-start.7 = (bf16[128,1024]{1,0:T(8,128)(2,1)S(1)}, bf16[128,1024]{1,0:T(8,128)(2,1)}, u32[]{:S(2)}) copy-start(bf16[128,1024]{1,0:T(8,128)(2,1)} %copy-done.6) | copy-start | bytes 786436
  301.8 63.1 %copy-start.9 = (bf16[128,1024]{1,0:T(8,128)(2,1)S(1)}, bf16[128,1024]{1,0:T(8,128)(2,1)}, u32[]{:S(2)}) copy-start(bf16[128,1024]{1,0:T(8,128)(2,1)} %copy-done.8) | copy-start | bytes 786436
  460.7 9.2 %all-to-all-start.3 = ((bf16[4,48,256]{2,1,0:T(8,128)(2,1)}), bf16[4,48,256]{2,1,0:T(8,128)(2,1)S(1)}, u32[]{:S(2)}, u32[]{:S(2)}) async-start(bf16[4,48,256]{2,1,0:T(8,128)(2,1)} %bitcast.46), calls=%async_computation.4 | async-start | bytes 196608 | tf_op jit(solution)/shard_map/all_to_all | solution.py:81
  (20 other events, 19.3 us)
Sparse Core Ops, SparseCore 0:
  301.9 157.1 reduce-scatter.1
